TPU v7x, 16 devices: a 4x2x1 block of a 4x4x8 slice. The times are simulated.
16 devices in a mesh: dp: 2 (over y, z), tp: 8 (over x, core).
Axes of the slice: x: 4, y: 2, z: 1, core: 2. Of those that a mesh axis runs over, the one named last changes fastest.
The devices are a block of a 4x4x8 slice.
Arguments:
- act_in: bfloat16 [512, 5120], P('dp'), parts along dimension 0
- w_qkv: bfloat16 [2, 5120, 40, 3, 128], P(None, None, 'tp')
- w_out: bfloat16 [2, 40, 128, 5120], P(None, 'tp')
- w_up: bfloat16 [2, 5120, 20480], P(None, None, 'tp')
- w_down: bfloat16 [2, 20480, 5120], P(None, 'tp')
- gain_one: float32 [2, 5120], replicated
- gain_two: float32 [2, 5120], replicated
Outputs:
- output: bfloat16 [512, 5120], P('dp'), parts along dimension 0
There are 2 independent parts. A program takes and returns all parts, laid end to end along the dimension named above; an argument that names none is the same for every part.
All inputs are finite; a program needn't handle non-finite values.
Results may differ from a plain program's by a relative error of at most 0.0165387.
Values are sent between devices in bfloat16 or wider.
A program may use at most 768 MiB of HBM per device.

v0:
```python
import functools
import math

import jax
import jax.numpy as jnp
from jax import lax
from jax.experimental import pallas as pl
from jax.experimental.pallas import tpu as pltpu
from jax.sharding import PartitionSpec as P

F32 = jnp.float32
BF16 = jnp.bfloat16
SLOTS = 14
Q_SLOTS = (12, 13, 2, 3)
PAIR, M1R, M1L, M2R, M2L, M3R, M3L = 0, 4, 5, 6, 7, 8, 9
OWN_RA, OWN_RB, OWN_LA, OWN_LB, FWD_R, FWD_L = 10, 11, 12, 13, 14, 15
SH_OWN, SH_LA, SH_LB, SH_RA, SH_RB, SH_OA, SH_OB = 16, 17, 18, 19, 20, 21, 22
KINDS = 23
ORDER = (2, 3, 1, 0)
SPLIT = (M1R, M1L, M3R, M3L, OWN_RA, OWN_LB, FWD_R, FWD_L, SH_OA, SH_OB)
SELF, OTHER = 0, 1


def layer_kernel(
    num_layers, num_chips, heads, head_dim,
    x_hbm, wq, wo, w1, w2, g1, g2, out,
    xg, a_buf, pb, pr, sb, rb, qkv, o_buf, h_buf, gains, st, w,
    wsem, xsem, ssem, rsem,
):
    rows = xg.shape[2]
    bw = xg.shape[3]
    own = rows // 2
    hw = bw // 2
    model_dim = num_chips * bw
    tp = 2 * num_chips
    me = lax.axis_index("tp")
    chip = me // 2
    core = me % 2
    mine = pl.ds(pl.multiple_of(core * own, own), own)
    theirs = pl.ds(pl.multiple_of((1 - core) * own, own), own)
    scope = jax.named_scope

    def chip_at(r):
        return lax.rem(chip + r, num_chips)

    def block(r):
        return pl.ds(pl.multiple_of(chip_at(r) * bw, bw), bw)

    right = chip_at(1) * 2 + core
    left = chip_at(3) * 2 + core
    partner = chip * 2 + (1 - core)
    half_a = pl.ds(0, hw)
    half_b = pl.ds(hw, hw)

    def load(l, what, n, s):
        res = []

        def slab(t, r, col):
            res.append((wq.at[l, t, block(r), :], w.at[s, :, pl.ds(col, head_dim)]))

        if what == "q" and n < 4:
            for t in range(10):
                slab(t, n, t * head_dim)
        elif what == "q":
            for i in range(2):
                for t in range(5):
                    slab(10 + t, 2 * (n - 4) + i, i * hw + t * head_dim)
        elif what == "o":
            for i in range(2):
                res.append((wo.at[l, :, block(ORDER[2 * n + i])], w.at[s, pl.ds(i * hw, hw), :]))
        elif what == "u":
            res.append((w1.at[l, block(n % 4), pl.ds((n // 4) * bw, bw)], w.at[s]))
        else:
            res.append((w2.at[l, pl.ds((n % 2) * bw, bw), block(ORDER[n // 2])], w.at[s]))
        for a, b in res:
            pltpu.make_async_copy(a, b, wsem.at[s]).start()

    def load_next(l, what, n, s):
        @pl.when(l + 1 < num_layers)
        def _():
            load(l + 1, what, n, s)

    def wait_w(*slots):
        with scope("wwait"):
            for s in slots:
                pltpu.make_async_copy(w.at[s], w.at[s], wsem.at[s]).wait()

    part = own // 2

    def piece(p):
        return pl.ds(0, own) if p is None else pl.ds(p * part, part)

    def mine_of(p):
        return mine if p is None else pl.ds(pl.multiple_of(core * own + p * part, part), part)

    def msg(h, kind, p=None):
        n = 0 if p is None else p

        def rc(src, dst, dev):
            return pltpu.make_async_remote_copy(
                src_ref=src, dst_ref=dst, send_sem=ssem.at[h, kind, n], recv_sem=rsem.at[h, kind, n],
                device_id={"tp": dev}, device_id_type=pl.DeviceIdType.MESH,
            )

        def move(r_from, r_to, cols, dev):
            return rc(xg.at[h, r_from, mine_of(p), cols], xg.at[h, r_to, mine_of(p), cols], dev)

        if kind < 4:
            return rc(pb.at[h, kind, theirs, :], pr.at[h, kind], partner)
        if kind <= M3L:
            k = kind - M1R
            return rc(sb.at[h, k, piece(p), :], rb.at[h, k, piece(p), :], right if k % 2 == 0 else left)
        return move(*{
            OWN_RA: (0, 3, half_a, right), OWN_RB: (0, 3, half_b, right),
            OWN_LA: (0, 1, half_a, left), OWN_LB: (0, 1, half_b, left),
            FWD_R: (3, 2, half_a, right), FWD_L: (1, 2, half_b, left),
            SH_OWN: (0, 0, pl.ds(0, bw), partner),
            SH_LA: (3, 3, half_a, partner), SH_LB: (3, 3, half_b, partner),
            SH_RA: (1, 1, half_a, partner), SH_RB: (1, 1, half_b, partner),
            SH_OA: (2, 2, half_a, partner), SH_OB: (2, 2, half_b, partner),
        }[kind])

    def send_pair(h, d):
        pltpu.make_async_remote_copy(
            src_ref=pb.at[h, d, theirs, :], dst_ref=pr.at[h, d], send_sem=ssem.at[h, d, 0], recv_sem=rsem.at[h, d, 0],
            device_id={"tp": partner}, device_id_type=pl.DeviceIdType.MESH,
        ).start()

    def send(h, *kinds, p=None):
        for kind in kinds:
            msg(h, kind, p).start()

    def recv(h, *kinds, p=None):
        for kind in kinds:
            with scope("recv%d" % kind):
                msg(h, kind, p).wait_recv()

    def pair_sum(h, d, cols, p=None):
        return pb[h, d, mine_of(p), cols].astype(F32) + pr[h, d, piece(p), cols].astype(F32)

    def ev1(h):
        recv(h, PAIR + 2)
        for p in range(2):
            sb[h, 0, piece(p), :] = pair_sum(h, 2, half_a, p).astype(BF16)
            sb[h, 1, piece(p), :] = pair_sum(h, 2, half_b, p).astype(BF16)
            send(h, M1R, M1L, p=p)

    def ev2_left(h):
        recv(h, PAIR + 3)
        sb[h, 3] = pair_sum(h, 3, half_a).astype(BF16)
        send(h, M2L)

    def ev2_right(h):
        recv(h, PAIR + 1)
        sb[h, 2] = pair_sum(h, 1, half_b).astype(BF16)
        send(h, M2R)

    def ev3(h):
        for p in range(2):
            recv(h, M1R, p=p)
            sb[h, 4, piece(p), :] = (pair_sum(h, 1, half_a, p) + rb[h, 0, piece(p), :].astype(F32)).astype(BF16)
            send(h, M3R, p=p)
            recv(h, M1L, p=p)
            sb[h, 5, piece(p), :] = (pair_sum(h, 3, half_b, p) + rb[h, 1, piece(p), :].astype(F32)).astype(BF16)
            send(h, M3L, p=p)

    def ev4(h):
        recv(h, PAIR + 0, M2L, M2R)

        def own_sum(cols, plain, summed, p):
            xg[h, 0, mine_of(p), cols] = (xg[h, 0, mine_of(p), cols].astype(F32) + (
                pair_sum(h, 0, cols, p) + rb[h, plain, piece(p), :].astype(F32)
                + rb[h, summed, piece(p), :].astype(F32))).astype(BF16)

        for p in range(2):
            recv(h, M3R, p=p)
            own_sum(half_a, 3, 4, p)
            send(h, OWN_RA, p=p)
            recv(h, M3L, p=p)
            own_sum(half_b, 2, 5, p)
            send(h, OWN_LB, p=p)
        send(h, OWN_LA, OWN_RB, SH_OWN)

    def ev5(h):
        for p in range(2):
            recv(h, OWN_RA, p=p)
            send(h, FWD_R, p=p)
            recv(h, OWN_LB, p=p)
            send(h, FWD_L, p=p)
        send(h, SH_LA, SH_RB)

    def ev6(h):
        recv(h, OWN_LA)
        send(h, SH_RA)
        recv(h, OWN_RB)
        send(h, SH_LB)

    def ev7(h):
        for p in range(2):
            recv(h, FWD_R, p=p)
            send(h, SH_OA, p=p)
            recv(h, FWD_L, p=p)
            send(h, SH_OB, p=p)

    def ev_near(h):
        recv(h, SH_OWN, SH_LA, SH_LB, SH_RA, SH_RB)

    def ev_near_stats(h):
        ev_near(h)
        near_stats(h)

    def ev8(h):
        for p in range(2):
            recv(h, SH_OA, SH_OB, p=p)
        with scope("sent"):
            for kind in range(KINDS):
                for p in (0, 1) if kind in SPLIT else (None,):
                    msg(h, kind, p).wait_send()

    def x_copy(h, r):
        src = x_hbm.at[pl.ds(pl.multiple_of(h * rows, rows), rows), block(r)]
        return pltpu.make_async_copy(src, xg.at[h, r], xsem.at[h, r])

    tiles = bw // 128

    def x_tile(h, r, t):
        return xg[h, r, :, t * 128:(t + 1) * 128].astype(F32)

    def block_stats(h, r):
        total = x_tile(h, r, 0)
        for t in range(1, tiles):
            total = total + x_tile(h, r, t)
        mean = jnp.sum(total, axis=1, keepdims=True) * (1.0 / bw)
        sq = jnp.zeros((rows, 128), F32)
        for t in range(tiles):
            d = x_tile(h, r, t) - mean
            sq = sq + d * d
        m2 = jnp.sum(sq, axis=1, keepdims=True)
        st[r, 0] = jnp.broadcast_to(mean, (rows, 128))
        st[r, 1] = jnp.broadcast_to(m2, (rows, 128))

    def near_stats(h):
        def one(n, c):
            block_stats(h, n + n // 2)
            return c

        with scope("stats"):
            lax.fori_loop(0, num_chips - 1, one, 0)

    def normalise(l, h, which):
        with scope("norm"):
            block_stats(h, 2)
            mean = (st[0, 0] + st[1, 0] + st[2, 0] + st[3, 0]) * (1.0 / num_chips)
            m2 = st[0, 1] + st[1, 1] + st[2, 1] + st[3, 1]
            for r in range(num_chips):
                d = st[r, 0] - mean
                m2 = m2 + bw * (d * d)
            rstd = lax.rsqrt(m2 * (1.0 / model_dim) + 1e-5)

            def scaled(r, c):
                for t in range(tiles):
                    g = gains[which, l, r, :, t * 128:(t + 1) * 128]
                    a_buf[r, :, t * 128:(t + 1) * 128] = ((x_tile(h, r, t) - mean) * rstd * g).astype(BF16)
                return c

            lax.fori_loop(0, num_chips, scaled, 0)

    def dot_all(lhs, rhs):
        return sum(jnp.dot(a, b, preferred_element_type=F32) for a, b in zip(lhs, rhs))

    def attn_steps(l, h):
        my_rows = pl.ds(pl.multiple_of(h * rows, rows), rows)

        def ln():
            @pl.when(l == 0)
            def _():
                for r in range(num_chips):
                    x_copy(h, r).wait()
                near_stats(h)

            normalise(l, h, 0)

            @pl.when(l + h == 0)
            def _():
                load(0, "q", 4, 4)
                load(0, "q", 5, 5)
                load(0, "o", 0, 6)
                load(0, "o", 1, 7)

        def qkv_main():
            @pl.when(h == 0)
            def _():
                wait_w(*Q_SLOTS)

            with scope("mm_qkv"):
                for first, count in ((0, 4), (4, 4), (8, 2)):
                    part = dot_all([a_buf[r] for r in range(4)],
                                   [w[s, :, pl.ds(first * head_dim, count * head_dim)] for s in Q_SLOTS])
                    for t in range(count):
                        qkv[first + t, my_rows, :] = part[:, t * head_dim:(t + 1) * head_dim].astype(BF16)

            @pl.when(h == 1)
            def _():
                for r in range(4):
                    load(l, "u", 4 + r, r)
                load_next(l, "q", 0, Q_SLOTS[0])
                load_next(l, "q", 1, Q_SLOTS[1])

            @pl.when(l + h == 0)
            def _():
                for r in range(4):
                    load(0, "u", r, 8 + r)

        def qkv_rest():
            @pl.when(h == 0)
            def _():
                wait_w(4, 5)

            with scope("mm_qkv2"):
                for first, count in ((0, 4), (4, 1)):
                    part = dot_all([a_buf[r] for r in range(4)],
                                   [w[4 + r // 2, :, pl.ds((r % 2) * hw + first * head_dim, count * head_dim)]
                                    for r in range(4)])
                    for t in range(count):
                        qkv[10 + first + t, my_rows, :] = part[:, t * head_dim:(t + 1) * head_dim].astype(BF16)

            @pl.when(h == 1)
            def _():
                load(l, "d", 0, 4)
                load(l, "d", 1, 5)

        def attend_half(static_h):
            at = pl.ds(static_h * rows, rows)
            shape = (rows, 2 * rows)
            q_pos = static_h * rows + lax.broadcasted_iota(jnp.int32, shape, 0)
            keep = lax.broadcasted_iota(jnp.int32, shape, 1) <= q_pos
            scale = 1.0 / math.sqrt(head_dim)
            with scope("attn"):
                for n in range(heads):
                    s = lax.dot_general(qkv[3 * n, at, :], qkv[3 * n + 1], (((1,), (1,)), ((), ())),
                                        preferred_element_type=F32) * scale
                    s = jnp.where(keep, s, -1e30)
                    p = jnp.exp(s - jnp.max(s, axis=1, keepdims=True))
                    total = jnp.sum(p, axis=1, keepdims=True)
                    mix = jnp.dot(p.astype(BF16), qkv[3 * n + 2], preferred_element_type=F32)
                    o_buf[:, n * head_dim:(n + 1) * head_dim] = (mix / total).astype(BF16)

        def attend():
            for static_h in range(2):
                pl.when(h == static_h)(functools.partial(attend_half, static_h))

        def prod(n):
            d = ORDER[n]
            s = 6 + n // 2
            if n % 2 == 0:
                @pl.when(h == 0)
                def _():
                    wait_w(s)

            with scope("mm_out"):
                pb[h, d] = jnp.dot(o_buf[...], w[s, pl.ds((n % 2) * hw, hw), :],
                                   preferred_element_type=F32).astype(BF16)
            send(h, PAIR + d)
            if n % 2 == 1:
                @pl.when(h == 1)
                def _():
                    load(l, "d", 2 + n // 2, s)

        return [ln, qkv_main, qkv_rest, attend] + [functools.partial(prod, n) for n in range(4)]

    def mlp_steps(l, h):
        def ln():
            normalise(l, h, 1)

        def up(n):
            base = 8 + n * (4 * h - 8)

            @pl.when((h == 0) | (n == 1))
            def _():
                wait_w(*[base + r for r in range(4)])

            with scope("mm_up"):
                part = dot_all([a_buf[r] for r in range(4)], [w[base + r] for r in range(4)])
                h_buf[n] = jax.nn.gelu(part, approximate=True).astype(BF16)

            @pl.when(h == 1 - n)
            def _():
                for r in range(4):
                    load(l, "d", 4 + r, base + r)

            @pl.when(h * n == 1)
            def _():
                load_next(l, "q", 4, 4)
                load_next(l, "q", 5, 5)
                load_next(l, "o", 0, 6)
                load_next(l, "o", 1, 7)

        def prod(n):
            d = 2 + n + (n // 2) * (1 - 2 * n)
            s0 = lax.rem(4 + 2 * n, 8)
            s1 = 2 * n + 4 * (n // 2)
            s = s0 + h * (s1 - s0)
            wait_w(s, s + 1)
            with scope("mm_down"):
                part = dot_all([h_buf[0], h_buf[1]], [w[s], w[s + 1]])
                pb[h, d] = part.astype(BF16)
            send_pair(h, d)
            for k in range(4):
                for i in range(2):
                    @pl.when((n == k) & (h == 0))
                    def _():
                        if k < 2:
                            load(l, "u", 4 + 2 * k + i, s0 + i)
                        else:
                            load(l, "d", 2 * (k - 2) + i, s0 + i)

                    @pl.when((n == k) & (h == 1))
                    def _():
                        if k < 2:
                            if k == 1:
                                load_next(l, "q", 2 + i, Q_SLOTS[2 + i])
                        else:
                            load_next(l, "u", 2 * (k - 2) + i, s1 + i)

        return ln, up, prod

    def run_attn(l, h, plan):
        for n, step in enumerate(attn_steps(l, h)):
            step()
            for whose, ev in plan.get(n, ()):
                if whose == SELF:
                    ev(h)
                else:
                    pl.when(l + h > 0)(functools.partial(ev, 1 - h))

    def run_mlp(l, h, plan):
        ln, up, prod = mlp_steps(l, h)

        def events(n, k, at):
            for whose, ev in plan.get(at, ()):
                pl.when(n == k)(functools.partial(ev, h if whose == SELF else 1 - h))

        def up_step(n, c):
            up(n)
            for k in range(2):
                events(n, k, 1 + k)
            return c

        def prod_step(n, c):
            prod(n)
            for k in range(3):
                events(n, k, 3 + k)
            return c

        ln()
        lax.fori_loop(0, 2, up_step, 0)
        lax.fori_loop(0, num_chips, prod_step, 0)
        for whose, ev in plan[6]:
            ev(h if whose == SELF else 1 - h)

    def put_out(h):
        with scope("put"):
            for r in range(num_chips):
                out[pl.ds(h * rows, rows), block(r)] = xg[h, r]

    for r in range(num_chips):
        x_copy(0, r).start()
    load(0, "q", 0, Q_SLOTS[0])
    load(0, "q", 1, Q_SLOTS[1])
    barrier = pltpu.get_barrier_semaphore()
    for n in range(1, tp):
        pl.semaphore_signal(barrier, inc=1, device_id={"tp": lax.rem(me + n, tp)},
                            device_id_type=pl.DeviceIdType.MESH)
    qkv[...] = jnp.zeros_like(qkv)
    for k, gain in enumerate((g1, g2)):
        for l in range(num_layers):
            for r in range(num_chips):
                gains[k, l, r] = gain[pl.ds(l, 1), block(r)]
    for r in range(num_chips):
        x_copy(1, r).start()
    for r in range(2, 4):
        load(0, "q", r, Q_SLOTS[r])
    with scope("bar"):
        pl.semaphore_wait(barrier, tp - 1)

    def layer(l, c):
        def attn_half(h, c):
            run_attn(l, h, {
                1: [(OTHER, ev4)],
                5: [(OTHER, ev5)],
                6: [(SELF, ev1), (OTHER, ev6)],
                7: [(SELF, ev2_left), (SELF, ev2_right), (OTHER, ev_near_stats), (OTHER, ev7), (SELF, ev3), (OTHER, ev8)],
            })
            return c

        def mlp_half(h, c):
            run_mlp(l, h, {
                1: [(OTHER, ev4)],
                3: [(OTHER, ev5)],
                4: [(SELF, ev1)],
                5: [(OTHER, ev6), (SELF, ev2_left)],
                6: [(SELF, ev2_right), (OTHER, ev_near_stats), (OTHER, ev7), (SELF, ev3), (OTHER, ev8)],
            })
            return c

        lax.fori_loop(0, 2, attn_half, 0)
        lax.fori_loop(0, 2, mlp_half, 0)
        return c

    lax.fori_loop(0, num_layers, layer, 0)
    ev4(1)
    put_out(0)
    for ev in (ev5, ev6, ev_near, ev7, ev8):
        ev(1)
    put_out(1)


def solution(mesh):
    tp = mesh.shape["tp"]
    num_chips = tp // 2

    def device_fn(act_in, w_qkv, w_out, w_up, w_down, gain_one, gain_two):
        seq, model_dim = act_in.shape
        num_layers, _, heads, _, head_dim = w_qkv.shape
        ffn = w_up.shape[2]
        bw = model_dim // num_chips
        half, hw = seq // 2, bw // 2
        wq = jnp.transpose(w_qkv, (0, 2, 3, 1, 4)).reshape(num_layers, heads * 3, model_dim, head_dim)
        wo = w_out.reshape(num_layers, heads * head_dim, model_dim)
        vmem = pl.BlockSpec(memory_space=pltpu.VMEM)
        hbm = pl.BlockSpec(memory_space=pl.ANY)
        return pl.pallas_call(
            functools.partial(layer_kernel, num_layers, num_chips, heads, head_dim),
            out_shape=pltpu.VMEM((seq, model_dim), BF16),
            in_specs=[hbm] * 5 + [vmem] * 2,
            out_specs=vmem,
            scratch_shapes=[
                pltpu.VMEM((2, num_chips, half, bw), BF16),
                pltpu.VMEM((num_chips, half, bw), BF16),
                pltpu.VMEM((2, num_chips, half, bw), BF16),
                pltpu.VMEM((2, num_chips, half // 2, bw), BF16),
                pltpu.VMEM((2, 6, half // 2, hw), BF16),
                pltpu.VMEM((2, 6, half // 2, hw), BF16),
                pltpu.VMEM((heads * 3, seq, head_dim), BF16),
                pltpu.VMEM((half, heads * head_dim), BF16),
                pltpu.VMEM((ffn // bw, half, bw), BF16),
                pltpu.VMEM((2, num_layers, num_chips, 1, bw), F32),
                pltpu.VMEM((num_chips, 2, half, 128), F32),
                pltpu.VMEM((SLOTS, bw, bw), BF16),
                pltpu.SemaphoreType.DMA((SLOTS,)),
                pltpu.SemaphoreType.DMA((2, num_chips)),
                pltpu.SemaphoreType.DMA((2, KINDS, 2)),
                pltpu.SemaphoreType.DMA((2, KINDS, 2)),
            ],
            compiler_params=pltpu.CompilerParams(
                collective_id=0, has_side_effects=True, vmem_limit_bytes=60 * 2 ** 20),
            name="layers",
        )(act_in, wq, wo, w_up, w_down, gain_one, gain_two)

    return jax.shard_map(
        device_fn,
        mesh=mesh,
        in_specs=(
            P("dp", None),
            P(None, None, "tp", None, None),
            P(None, "tp", None, None),
            P(None, None, "tp"),
            P(None, "tp", None),
            P(None, None),
            P(None, None),
        ),
        out_specs=P("dp", None),
        check_vma=False,
    )
```

profile of v0, /device:TPU:113, one launch (start us, length us, event | category | flops | bytes accessed | tf_op | source)
XLA Modules:
  0.0 130.2 jit_solution(8278748470048973735)
XLA Ops:
  0.0 128.7 %layers.1 = bf16[256,5120]{1,0:T(8,128)(2,1)S(1)} custom-call(bf16[256,5120]{1,0:T(8,128)(2,1)} %x_hbm.1, bf16[2,15,5120,128]{3,2,1,0:T(8,128)(2,1)} %bitcast.4, bf16[2,640,5120]{2,1,0:T(8,128)(2,1)} %bitcast.5, bf16[2,5120,2560]{2,1,0:T(8,128)(2,1)} %w1.1, bf16[2,2560,5120]{2,1,0:T(8,128)(2,1)} %w2.1, f32[2,5120]{1,0:T(2,128)} %g1.1, f32[2,5120]{1,0:T(2,128)} %g2.1), custom_call_target="tpu_custom_call" | custom-call | tf_op jit(solution)/shard_map/layers/pallas_call | solution.py:532
  128.7 1.5 %copy.9 = bf16[256,5120]{1,0:T(8,128)(2,1)} copy(bf16[256,5120]{1,0:T(8,128)(2,1)S(1)} %layers.1) | data formatting | bytes 5242880
where the time goes:
time: 130 us
  Pallas kernels  129 us (99%)
  local copies, waits for them, and re-layouts  1.49 us (1%)
    pallas_call x1, Pallas kernels, device_fn(): pl.pallas_call(functools.partial(layer_kernel, num_layers, num_chips, hea...  129 us

commit v1 on v0

--- a/solution.py
+++ b/solution.py
@@ -487,8 +487,7 @@
         def attn_half(h, c):
             run_attn(l, h, {
                 1: [(OTHER, ev4)],
-                5: [(OTHER, ev5)],
-                6: [(SELF, ev1), (OTHER, ev6)],
+                6: [(OTHER, ev5), (SELF, ev1), (OTHER, ev6)],
                 7: [(SELF, ev2_left), (SELF, ev2_right), (OTHER, ev_near_stats), (OTHER, ev7), (SELF, ev3), (OTHER, ev8)],
             })
             return c
@@ -496,8 +495,7 @@
         def mlp_half(h, c):
             run_mlp(l, h, {
                 1: [(OTHER, ev4)],
-                3: [(OTHER, ev5)],
-                4: [(SELF, ev1)],
+                4: [(OTHER, ev5), (SELF, ev1)],
                 5: [(OTHER, ev6), (SELF, ev2_left)],
                 6: [(SELF, ev2_right), (OTHER, ev_near_stats), (OTHER, ev7), (SELF, ev3), (OTHER, ev8)],
             })

time: 130 us -> 131 us (level)
  no operation moved by 1% of the time
where the time goes in v1:
time: 131 us
  Pallas kernels  130 us (99%)
  local copies, waits for them, and re-layouts  1.49 us (1%)
    pallas_call x1, Pallas kernels, device_fn(): pl.pallas_call(functools.partial(layer_kernel, num_layers, num_chips, hea...  130 us

profile of v1, /device:TPU:113, one launch (start us, length us, event | category | flops | bytes accessed | tf_op | source)
XLA Modules:
  0.0 131.3 jit_solution(7620559326002545801)
XLA Ops:
  0.0 129.8 %layers.1 = bf16[256,5120]{1,0:T(8,128)(2,1)S(1)} custom-call(bf16[256,5120]{1,0:T(8,128)(2,1)} %x_hbm.1, bf16[2,15,5120,128]{3,2,1,0:T(8,128)(2,1)} %bitcast.4, bf16[2,640,5120]{2,1,0:T(8,128)(2,1)} %bitcast.5, bf16[2,5120,2560]{2,1,0:T(8,128)(2,1)} %w1.1, bf16[2,2560,5120]{2,1,0:T(8,128)(2,1)} %w2.1, f32[2,5120]{1,0:T(2,128)} %g1.1, f32[2,5120]{1,0:T(2,128)} %g2.1), custom_call_target="tpu_custom_call" | custom-call | tf_op jit(solution)/shard_map/layers/pallas_call | solution.py:530
  129.8 1.5 %copy.9 = bf16[256,5120]{1,0:T(8,128)(2,1)} copy(bf16[256,5120]{1,0:T(8,128)(2,1)S(1)} %layers.1) | data formatting | bytes 5242880
